TPU v7x, 512 devices: a whole 4x4x16 slice. The times are simulated.
512 devices in a mesh: row: 32 (over x_lo, z), col: 16 (over x_hi, y, core).
Axes of the slice: x: 4 (x_hi: 2, x_lo: 2; x = x_hi * 2 + x_lo), y: 4, z: 16, core: 2. Of those that a mesh axis runs over, the one named last changes fastest.
Arguments:
- tokens: bfloat16 [256, 12288], P('row', 'col'), may hold values from -6 to 6
- past_tokens: bfloat16 [256, 12288], P('row', 'col'), may hold values from -6 to 6
- out_grad: bfloat16 [256, 12288], P('row', 'col'), may hold values from -3 to 3
- w_in: bfloat16 [12288, 24576], P('col', 'row'), may hold values from -0.0546875 to 0.0546875
- w_out: bfloat16 [24576, 12288], P('row', 'col'), may hold values from -0.0390625 to 0.0390625
Outputs:
- layer_out: bfloat16 [256, 12288], P('row', 'col')
- input_grad: bfloat16 [256, 12288], P('row', 'col')
- grad_w_in: bfloat16 [12288, 24576], P('col', 'row')
- grad_w_out: bfloat16 [24576, 12288], P('row', 'col')
All inputs are finite; a program needn't handle non-finite values.
Results may differ from a plain program's by a relative error of at most 0.005.
Values may be sent and summed in bfloat16 or wider, within the bound.
A program may use at most 64 MiB of HBM per device.

v0:
```python
import jax
import jax.numpy as jnp
from jax import lax
from jax.sharding import Mesh
from jax.sharding import PartitionSpec as P

ROW = ("row_0", "row_1")


def in_order(pieces, dim):
    pieces = jnp.moveaxis(pieces, 0, dim)
    shape = pieces.shape
    return pieces.reshape(*shape[:dim], shape[dim] * shape[dim + 1], *shape[dim + 2 :])


def stacked_from(shard, axes, order):
    pieces = shard[None]
    for k in order:
        pieces = lax.all_gather(pieces, axes[k], axis=0, tiled=True)
    carried = [lax.axis_size(axes[k]) for k in reversed(order)]
    pieces = pieces.reshape(*carried, *shard.shape)
    turned = sorted(range(len(order)), key=lambda place: order[len(order) - 1 - place])
    return pieces.transpose(*turned, *range(len(order), pieces.ndim)).reshape(-1, *shard.shape)


def gather_axes(shard, axes, order, dim):
    return in_order(stacked_from(shard, axes, order), dim)


def cut_along(shard, dim, length):
    shape = shard.shape
    pieces = shard.reshape(*shape[:dim], length, shape[dim] // length, *shape[dim + 1 :])
    return jnp.moveaxis(pieces, dim, 0)


def sent_and_summed(shard, axis, dim):
    pieces = cut_along(shard, dim, lax.axis_size(axis))
    arrived = lax.all_to_all(pieces, axis, split_axis=0, concat_axis=0, tiled=True)
    return arrived.sum(axis=0)


def sent_to_all(shard, axis):
    copies = jnp.broadcast_to(shard, (lax.axis_size(axis), *shard.shape))
    return lax.all_to_all(copies, axis, split_axis=0, concat_axis=0, tiled=True)


def gathered_copies(shard, axis, dim):
    return in_order(sent_to_all(shard, axis), dim)


def sent_together(arrays, axis, dim, along):
    both = jnp.concatenate(arrays, axis=along)
    out, at, gathered = (lax.all_gather(both, axis, axis=dim, tiled=True), 0, [])
    for a in arrays:
        gathered.append(lax.slice_in_dim(out, at, at + a.shape[along], axis=along))
        at += a.shape[along]
    return tuple(gathered)


def in_one_piece(arrays, axis, dim, along):
    widths = [a.shape[along] for a in arrays]
    both = jnp.concatenate(arrays, axis=along)
    out = lax.psum_scatter(both, axis, scatter_dimension=dim, tiled=True)
    return tuple(jnp.split(out, [sum(widths[:k]) for k in range(1, len(widths))], axis=along))


def gelu_parts(pre):
    cdf = 0.5 * (1.0 + jax.scipy.special.erf(pre * 0.7071067811865476))
    slope = cdf + pre * jnp.exp(-0.5 * pre * pre) * 0.3989422804014327
    return (pre * cdf, slope)


def local(tokens, past_tokens, out_grad, w_in, w_out):
    pre_part = jnp.dot(
        gather_axes(tokens, ROW, (0, 1), 0), w_in, preferred_element_type=jnp.float32
    )
    pre_share = sent_and_summed(pre_part, "col", 0)
    hidden_share = gelu_parts(pre_share)[0].astype(jnp.bfloat16)
    hidden_all = gathered_copies(hidden_share, "col", 0)
    block = hidden_all
    layer_out = sent_and_summed(
        jnp.dot(block, w_out, preferred_element_type=jnp.float32), ROW, 0
    ).astype(jnp.bfloat16)
    past_all, grad_all = sent_together((past_tokens, out_grad), ROW, 0, 1)
    past_part = jnp.dot(past_all, w_in, preferred_element_type=jnp.float32)
    back_part = lax.dot_general(
        grad_all, w_out, (((1,), (1,)), ((), ())), preferred_element_type=jnp.float32
    )
    past_share, back_share = in_one_piece((past_part, back_part), "col", 0, 1)
    act_share, slope = gelu_parts(past_share)
    act_local = act_share.astype(jnp.bfloat16)
    grad_local = (back_share * slope).astype(jnp.bfloat16)
    act_all, hidden_grad = sent_together((act_local, grad_local), "col", 0, 1)
    grad_w_out = lax.dot_general(
        act_all, grad_all, (((0,), (0,)), ((), ())), preferred_element_type=jnp.float32
    ).astype(jnp.bfloat16)
    grad_w_in = lax.dot_general(
        past_all, hidden_grad, (((0,), (0,)), ((), ())), preferred_element_type=jnp.float32
    ).astype(jnp.bfloat16)
    block = hidden_grad
    input_grad = sent_and_summed(
        lax.dot_general(block, w_in, (((1,), (1,)), ((), ())), preferred_element_type=jnp.float32),
        ROW,
        0,
    ).astype(jnp.bfloat16)
    return (layer_out, input_grad, grad_w_in, grad_w_out)


def solution(mesh):
    split = Mesh(mesh.devices.reshape(2, 16, mesh.shape["col"]), ("row_0", "row_1", "col"))
    return jax.shard_map(
        local,
        mesh=split,
        in_specs=(P(ROW, "col"), P(ROW, "col"), P(ROW, "col"), P("col", ROW), P(ROW, "col")),
        out_specs=(P(ROW, "col"), P(ROW, "col"), P("col", ROW), P(ROW, "col")),
        check_vma=False,
    )
```

profile of v0, /device:TPU:1, one launch (start us, length us, event | category | flops | bytes accessed | tf_op | source)
XLA Modules:
  0.0 311.5 jit_solution(4100335702246159757)
XLA Ops:
  7.2 0.0 copy-start
  7.2 4.2 %all-gather = bf16[16,768]{1,0:T(8,128)(2,1)S(1)} all-gather(bf16[8,768]{1,0:T(8,128)(2,1)} %param.5), channel_id=2, replica_groups=mesh['row_0'=2,'row_1'=16,'col'=16] {'row_0'}, dimensions={0}, use_global_device_ids=true | all-gather | bytes 36864 | tf_op jit(solution)/shard_map/all_gather | solution.py:19
  11.4 31.4 %all_gather.13 = bf16[32,8,768]{2,1,0:T(8,128)(2,1)S(1)} all-gather(bf16[2,8,768]{2,1,0:T(8,128)(2,1)S(1)} %bitcast.22), channel_id=1, replica_groups=mesh['row_0'=2,'row_1'=16,'col'=16] {'row_1'}, dimensions={0}, use_global_device_ids=true | all-gather | bytes 417792 | tf_op jit(solution)/shard_map/all_gather | solution.py:19
  42.8 0.0 copy-done
  42.9 1.4 fusion.2
  44.2 15.3 %all-to-all-start = ((f32[16,16,768]{2,1,0:T(8,128)}), f32[16,16,768]{2,1,0:T(8,128)}, u32[]{:S(2)}, u32[]{:S(2)}) async-start(f32[16,16,768]{2,1,0:T(8,128)} %fusion.2), calls=%async_computation | async-start | bytes 1572864 | tf_op jit(solution)/shard_map/all_to_all | solution.py:38
  59.5 50.4 %all_gather.14 = bf16[256,1536]{1,0:T(8,128)(2,1)S(1)} all-gather(bf16[8,1536]{1,0:T(8,128)(2,1)S(1)} %pad_maximum_fusion.2), channel_id=1, replica_groups=mesh['row_0'=2,'row_1'=16,'col'=16] {'row_0','row_1'}, dimensions={0}, use_global_device_ids=true | all-gather | bytes 811008 | tf_op jit(solution)/shard_map/all_gather | solution.py:53
  109.9 1.4 fusion.11
  111.3 0.0 all-to-all-done
  111.3 1.3 reduce_sum.27
  112.6 0.8 broadcast_in_dim.7
  113.4 20.5 %all-to-all-start.1 = ((bf16[16,16,768]{2,1,0:T(8,128)(2,1)}), bf16[16,16,768]{2,1,0:T(8,128)(2,1)S(1)}, u32[]{:S(2)}, u32[]{:S(2)}) async-start(bf16[16,16,768]{2,1,0:T(8,128)(2,1)} %broadcast_in_dim.7), calls=%async_computation.1 | async-start | bytes 786432 | tf_op jit(solution)/shard_map/all_to_all | solution.py:44
  133.9 0.0 reduce-scatter.2.cloned.1.call-start
  134.0 0.0 copy-start.2
  134.0 0.5 fusion.8
  134.5 0.6 copy-done.2
  135.1 1.3 pad_maximum_fusion
  136.4 0.0 reduce-scatter.2.cloned.1.call-update
  136.5 7.2 %all-to-all-done.1 = bf16[16,16,768]{2,1,0:T(8,128)(2,1)S(1)} async-done(((bf16[16,16,768]{2,1,0:T(8,128)(2,1)}), bf16[16,16,768]{2,1,0:T(8,128)(2,1)S(1)}, u32[]{:S(2)}, u32[]{:S(2)}) %all-to-all-start.1) | async-done | bytes 393248 | tf_op jit(solution)/shard_map/all_to_all | solution.py:44
  143.7 1.4 fusion
  145.0 3.9 %all-to-all-start.2 = ((f32[32,8,768]{2,1,0:T(8,128)}), f32[32,8,768]{2,1,0:T(8,128)S(1)}, u32[]{:S(2)}, u32[]{:S(2)}) async-start(f32[32,8,768]{2,1,0:T(8,128)} %fusion), calls=%async_computation.2 | async-start | bytes 1572864 | tf_op jit(solution)/shard_map/all_to_all | solution.py:38
  148.9 72.1 %reduce-scatter.2.cloned.1.call-done = f32[16,1536]{1,0:T(8,128)} async-done(((f32[256,1536]{1,0:T(8,128)}), f32[16,1536]{1,0:T(8,128)}) %reduce-scatter.2.cloned.1.call-update) | async-done | bytes 98320 | tf_op jit(solution)/shard_map/reduce_scatter | solution.py:63
  221.1 0.9 multiply_convert_fusion
  222.0 26.1 %all_gather.15 = bf16[256,1536]{1,0:T(8,128)(2,1)S(1)} all-gather(bf16[16,1536]{1,0:T(8,128)(2,1)S(1)} %pad_maximum_fusion.1), channel_id=1, replica_groups=mesh['row_0'=2,'row_1'=16,'col'=16] {'col'}, dimensions={0}, use_global_device_ids=true | all-gather | bytes 835584 | tf_op jit(solution)/shard_map/all_gather | solution.py:53
  248.1 1.4 convolution_bitcast_fusion
  249.5 0.0 all-to-all-done.2
  249.5 13.2 %all-to-all-start.3 = ((f32[32,8,768]{2,1,0:T(8,128)}), f32[32,8,768]{2,1,0:T(8,128)}, u32[]{:S(2)}, u32[]{:S(2)}) async-start(f32[32,8,768]{2,1,0:T(8,128)} %convolution_bitcast_fusion), calls=%async_computation.4 | async-start | bytes 1572864 | tf_op jit(solution)/shard_map/all_to_all | solution.py:38
  262.7 1.5 convolution_convert_fusion
  264.2 1.5 convolution_convert_fusion.1
  265.7 0.7 reduce_sum.28
  266.4 36.4 %all-to-all-done.3 = f32[32,8,768]{2,1,0:T(8,128)} async-done(((f32[32,8,768]{2,1,0:T(8,128)}), f32[32,8,768]{2,1,0:T(8,128)}, u32[]{:S(2)}, u32[]{:S(2)}) %all-to-all-start.3) | async-done | bytes 786464 | tf_op jit(solution)/shard_map/all_to_all | solution.py:38
  302.8 1.8 reduce_sum.29
  (10 shorter events, 0.1 us)
Async XLA Ops:
  7.2 35.7 %copy-start = (bf16[768,768]{1,0:T(8,128)(2,1)S(1)}, bf16[768,768]{1,0:T(8,128)(2,1)}, u32[]{:S(2)}) copy-start(bf16[768,768]{1,0:T(8,128)(2,1)} %param.8) | copy-start | bytes 3538948
  44.2 15.3 %copy-start.3 = (bf16[8,768]{1,0:T(8,128)(2,1)S(1)}, bf16[8,768]{1,0:T(8,128)(2,1)}, u32[]{:S(2)}) copy-start(bf16[8,768]{1,0:T(8,128)(2,1)} %param.7) | copy-start | bytes 36868
  44.2 15.3 %copy-start.4 = (bf16[8,768]{1,0:T(8,128)(2,1)S(1)}, bf16[8,768]{1,0:T(8,128)(2,1)}, u32[]{:S(2)}) copy-start(bf16[8,768]{1,0:T(8,128)(2,1)} %param.6) | copy-start | bytes 36868
  44.2 67.1 %all-to-all-start = ((f32[16,16,768]{2,1,0:T(8,128)}), f32[16,16,768]{2,1,0:T(8,128)}, u32[]{:S(2)}, u32[]{:S(2)}) async-start(f32[16,16,768]{2,1,0:T(8,128)} %fusion.2), calls=%async_computation | async-start | bytes 1572864 | tf_op jit(solution)/shard_map/all_to_all | solution.py:38
  111.3 22.7 %copy-start.1 = (bf16[768,768]{1,0:T(8,128)(2,1)S(1)}, bf16[768,768]{1,0:T(8,128)(2,1)}, u32[]{:S(2)}) copy-start(bf16[768,768]{1,0:T(8,128)(2,1)} %param.9) | copy-start | bytes 3538948
  113.4 30.3 %all-to-all-start.1 = ((bf16[16,16,768]{2,1,0:T(8,128)(2,1)}), bf16[16,16,768]{2,1,0:T(8,128)(2,1)S(1)}, u32[]{:S(2)}, u32[]{:S(2)}) async-start(bf16[16,16,768]{2,1,0:T(8,128)(2,1)} %broadcast_in_dim.7), calls=%async_computation.1 | async-start | bytes 786432 | tf_op jit(solution)/shard_map/all_to_all | solution.py:44
  133.9 87.2 %reduce-scatter.2.cloned.1.call-start = ((), (), s32[]{:S(2)}) async-start(), calls=%async_computation.5 | async-start | bytes 1671168 | tf_op jit(solution)/shard_map/reduce_scatter | solution.py:63
  134.0 1.1 copy-start.2
  145.0 104.4 %all-to-all-start.2 = ((f32[32,8,768]{2,1,0:T(8,128)}), f32[32,8,768]{2,1,0:T(8,128)S(1)}, u32[]{:S(2)}, u32[]{:S(2)}) async-start(f32[32,8,768]{2,1,0:T(8,128)} %fusion), calls=%async_computation.2 | async-start | bytes 1572864 | tf_op jit(solution)/shard_map/all_to_all | solution.py:38
  249.5 53.3 %all-to-all-start.3 = ((f32[32,8,768]{2,1,0:T(8,128)}), f32[32,8,768]{2,1,0:T(8,128)}, u32[]{:S(2)}, u32[]{:S(2)}) async-start(f32[32,8,768]{2,1,0:T(8,128)} %convolution_bitcast_fusion), calls=%async_computation.4 | async-start | bytes 1572864 | tf_op jit(solution)/shard_map/all_to_all | solution.py:38
Sparse Core Ops, SparseCore 0:
  139.5 81.5 reduce-scatter.1
where the time goes:
time: 315 us; the launch traced here: 311 us
  waiting for transfers between devices  116 us (37%)
  blocking collectives  112 us (36%)
  starting transfers between devices  53 us (17%)
  between operations  14.1 us (4%)
  matrix products  9.04 us (3%)
  other arithmetic  5.96 us (2%)
    all_gather x2, blocking collectives, sent_together(): lax.all_gather(both, axis, axis=dim, tiled=True)  76.5 us
    reduce_scatter x1, waiting for transfers between devices, in_one_piece(): out = lax.psum_scatter(both, axis, scatter_dimension=dim, tiled=True)  72.1 us
    all_to_all x3, waiting for transfers between devices, sent_and_summed(): lax.all_to_all(pieces, axis, split_axis=0, concat_axis=0, tiled=True)  36.4 us
    all_gather x2, blocking collectives, stacked_from(): pieces = lax.all_gather(pieces, axes[k], axis=0, tiled=True)  35.6 us
    all_to_all x3, starting transfers between devices, sent_and_summed(): lax.all_to_all(pieces, axis, split_axis=0, concat_axis=0, tiled=True)  32.4 us
    all_to_all x1, starting transfers between devices, sent_to_all(): return lax.all_to_all(copies, axis, split_axis=0, concat_axis=0, tiled=True)  20.5 us
    all_to_all x1, waiting for transfers between devices, sent_to_all(): return lax.all_to_all(copies, axis, split_axis=0, concat_axis=0, tiled=True)  7.21 us
  transfers between devices with their start and end apart: 5, of which 3 were waited for; matrix products, arithmetic and copies ran while one was open for 3% of the time, Pallas kernels for 0%

commit v1 on v0

v1 whole, which is shorter than its diff:
```python
import functools

import jax
import jax.numpy as jnp
from jax import lax
from jax.experimental import pallas as pl
from jax.experimental.pallas import tpu as pltpu
from jax.sharding import PartitionSpec as P

MESH = pl.DeviceIdType.MESH
F32, BF16 = jnp.float32, jnp.bfloat16
NZ = 16


def gelu_parts(pre):
    cdf = 0.5 * (1.0 + lax.erf(pre * 0.7071067811865476))
    slope = cdf + pre * jnp.exp(-0.5 * pre * pre) * 0.3989422804014327
    return (pre * cdf, slope)


LANES = ((0, 0), (1, 0), (2, 0), (2, 1))
FAR = (0, 1, 0, 1)


def kernel(
    past_ref, grad_ref, tok_ref, win_hbm, wout_hbm,
    lay_ref, ing_ref, pall_ref, gall_ref, aall_ref, hall_ref,
    T, win, wout, Pf, Pb, Dr, S8, Cs, Cr, H,
    Rf, Xb, Xr, Sf, Sb, R1, Uf, Ub, R2,
    wsem, azs, azr, axs, axr, lsem,
    dss, drs, css, crs, hss, hrs, hds, hdr,
    xss, xrs, s1s, s1r, s2s, s2r,
):
    r, q = lax.axis_index("row"), lax.axis_index("col")
    xl, z = r // NZ, r % NZ
    ch, c = q // 2, q % 2
    xh, y = ch // 4, ch % 4
    xp = (1 - xl) * NZ + z
    qp = ch * 2 + (1 - c)

    def zrow(d):
        return xl * NZ + (z + d + NZ) % NZ

    def chip(k, sign=1):
        return ((xh + sign * (k // 4) + 2) % 2) * 4 + (y + sign * (k % 4) + 4) % 4

    def rcopy(src, dst, ss, rs, rr, qq):
        return pltpu.make_async_remote_copy(
            src_ref=src, dst_ref=dst, send_sem=ss, recv_sem=rs, device_id=(rr, qq), device_id_type=MESH
        )

    cw1 = pltpu.make_async_copy(win_hbm, win, wsem.at[0])
    cw2 = pltpu.make_async_copy(wout_hbm, wout, wsem.at[1])
    cw1.start()
    cw2.start()
    own = (past_ref, grad_ref, tok_ref)
    locs = [pltpu.make_async_copy(own[a], T.at[a, r], lsem.at[a]) for a in range(3)]
    for cp in locs:
        cp.start()

    barrier = pltpu.get_barrier_semaphore()
    rows = [zrow(d) for d in (1, -1, 2, -2, 4, -4, 8)] + [xp]
    for rr in rows:
        pl.semaphore_signal(barrier, inc=1, device_id=(rr, q), device_id_type=MESH)
    for qq in [chip(k) * 2 + c for k in range(1, 8)] + [qp]:
        pl.semaphore_signal(barrier, inc=1, device_id=(r, qq), device_id_type=MESH)
    pl.semaphore_wait(barrier, 16)

    def xcopy(src, a, slot_z, slot):
        return rcopy(src, T.at[a, slot], axs.at[a, slot_z], axr.at[a, slot_z], xp, q)

    def zcopy(src, a, slot, di, s, ln):
        return rcopy(src, T.at[a, slot], azs.at[di, s, ln], azr.at[di, s + 1, ln], zrow(1 - 2 * di), q)

    for a in (2, 0, 1):
        xcopy(own[a], a, z, r).start()
    for ln, (a, h) in enumerate(LANES):
        if h == 0:
            for di in range(2):
                zcopy(own[a], a, r, di, 0, ln).start()
    for ln, (a, h) in enumerate(LANES):
        if h == 1:
            xcopy(T.at[a, xp], a, z, xp).wait_recv()
            for di in range(2):
                zcopy(T.at[a, xp], a, xp, di, 0, ln).start()

    def arrive(s, far):
        for di in range(2):
            zz = (z - (1 - 2 * di) * s + 2 * NZ) % NZ
            for ln, (a, h) in enumerate(LANES):
                if far == 2 and FAR[ln] != di:
                    continue
                slot = (xl if h == 0 else 1 - xl) * NZ + zz
                zcopy(T.at[a, slot], a, slot, di, s - 1, ln).wait_recv()
                if far == 0 or (far == 1 and FAR[ln] == di):
                    zcopy(T.at[a, slot], a, slot, di, s, ln).start()
                if h == 0 and a != 2:
                    xcopy(T.at[a, slot], a, zz, slot).start()

    @pl.loop(1, 7)
    def _(s):
        arrive(s, 0)

    arrive(7, 1)
    arrive(8, 2)

    cw1.wait()
    cw2.wait()
    for cp in locs:
        cp.wait()

    def wait_x(a):
        @pl.loop(0, NZ)
        def _(zz):
            slot = (1 - xl) * NZ + zz
            xcopy(T.at[a, slot], a, zz, slot).wait_recv()

    def gathered(a):
        return T[a].astype(F32).reshape(256, 768).astype(BF16)

    def d2d(k):
        return rcopy(Pb.at[k, :, 1 - c], Dr.at[k], dss.at[k], drs.at[k], r, qp)

    def partial(k, part):
        part = part.reshape(8, 2, 16, 768)
        Pf[k] = part
        Pb[k] = part.astype(BF16)
        d2d(k).start()

    wait_x(0)
    x = gathered(0)
    pall_ref[...] = x
    partial(0, jnp.dot(x, win[...], preferred_element_type=F32))
    wait_x(1)
    x = gathered(1)
    gall_ref[...] = x
    partial(1, lax.dot_general(x, wout[...], (((1,), (1,)), ((), ())), preferred_element_type=F32))
    partial(2, jnp.dot(gathered(2), win[...], preferred_element_type=F32))

    def csend(k, j):
        return rcopy(Cs.at[k, chip(j)], Cr.at[k, j], css.at[k, j], crs.at[k, j], r, chip(j) * 2 + c)

    for k in range(3):
        d2d(k).wait_recv()
        sums = Pf[k, :, c] + Dr[k].astype(F32)
        S8[k] = sums
        Cs[k] = sums.astype(BF16)
        for j in range(1, 8):
            csend(k, j).start()

    def summed(k):
        total = S8[k, ch]
        for j in range(1, 8):
            csend(k, j).wait_recv()
        for j in range(1, 8):
            total = total + Cr[k, j].astype(F32)
        return total

    def hsend(k, j):
        return rcopy(H.at[k, ch, c], H.at[k, ch, c], hss.at[k, j], hrs.at[k, j], r, chip(j) * 2 + c)

    def hpass(k, j):
        src = H.at[k, chip(j, -1), c]
        return rcopy(src, src, hds.at[k, j], hdr.at[k, j], r, qp)

    def hpassed(k, j):
        src = H.at[k, chip(j, -1), 1 - c]
        return rcopy(src, src, hds.at[k, j], hdr.at[k, j], r, qp)

    def hrecv(k, j):
        src = H.at[k, chip(j, -1), c]
        return rcopy(src, src, hss.at[k, j], hrs.at[k, j], r, qp)

    def spread(k, value):
        H[k, ch, c] = value
        for j in range(1, 8):
            hsend(k, j).start()
        hpass(k, 0).start()

    act, slope = gelu_parts(summed(0))
    spread(0, act.astype(BF16))
    spread(1, (summed(1) * slope).astype(BF16))
    spread(2, gelu_parts(summed(2))[0].astype(BF16))
    for k in range(3):
        for j in (1, 3, 4, 2, 5, 7, 6):
            hrecv(k, j).wait_recv()
            hpass(k, j).start()

    def whole(k):
        for j in range(8):
            hpassed(k, j).wait_recv()
        return H[k].reshape(256, 768)

    def xsend(k):
        return rcopy(Xb.at[k, 1 - xl], Xr.at[k], xss.at[k], xrs.at[k], xp, q)

    def rpartial(k, part):
        part = part.reshape(2, NZ, 8, 768)
        Rf[k] = part
        Xb[k] = part.astype(BF16)
        xsend(k).start()

    aall_ref[...] = whole(0)
    x = whole(1)
    hall_ref[...] = x
    rpartial(0, lax.dot_general(x, win[...], (((1,), (1,)), ((), ())), preferred_element_type=F32))
    rpartial(1, jnp.dot(whole(2), wout[...], preferred_element_type=F32))

    STEP1 = ((1, -1, 2), (1, -1, -2))

    def send1(k, i):
        d = STEP1[k][i]
        return rcopy(Sb.at[k, :, (z + d + NZ) % 4], R1.at[k, i], s1s.at[k, i], s1r.at[k, i], zrow(d), q)

    for k in range(2):
        xsend(k).wait_recv()
        s = Rf[k, xl] + Xr[k].astype(F32)
        s = s.reshape(4, 4, 8, 768)
        Sf[k] = s
        Sb[k] = s.astype(BF16)
        for i in range(3):
            send1(k, i).start()

    def send2(k, i):
        d = 4 * i
        return rcopy(Ub.at[k, ((z + d) % NZ) // 4], R2.at[k, i], s2s.at[k, i], s2r.at[k, i], zrow(d), q)

    for k in range(2):
        u = Sf[k, :, z % 4]
        for i in range(3):
            send1(k, i).wait_recv()
        for i in range(3):
            u = u + R1[k, i].astype(F32)
        Uf[k] = u
        Ub[k] = u.astype(BF16)
        for i in range(1, 4):
            send2(k, i).start()

    outs = (ing_ref, lay_ref)
    for k in range(2):
        v = Uf[k, z // 4]
        for i in range(1, 4):
            send2(k, i).wait_recv()
        for i in range(1, 4):
            v = v + R2[k, i].astype(F32)
        outs[k][...] = v.astype(BF16)

    for k in range(2):
        xsend(k).wait_send()
        for i in range(3):
            send1(k, i).wait_send()
            send2(k, i + 1).wait_send()
    for k in range(3):
        d2d(k).wait_send()
        for j in range(1, 8):
            csend(k, j).wait_send()
            hsend(k, j).wait_send()
        for j in range(8):
            hpass(k, j).wait_send()
    for a in range(2):
        @pl.loop(0, NZ)
        def _(zz):
            slot = xl * NZ + zz
            xcopy(T.at[a, slot], a, zz, slot).wait_send()
    xcopy(T.at[2, r], 2, z, r).wait_send()

    for ln, (a, h) in enumerate(LANES):
        for di in range(2):
            n = 8 if FAR[ln] == di else 7

            @pl.loop(0, n)
            def _(s):
                zcopy(T.at[a, r], a, r, di, s, ln).wait_send()


def call(past, grad, tok, win, wout):
    vm = pl.BlockSpec(memory_space=pltpu.VMEM)
    hbm = pl.BlockSpec(memory_space=pl.ANY)
    V = pltpu.VMEM
    D = lambda *s: pltpu.SemaphoreType.DMA(s)
    blk = jax.ShapeDtypeStruct((8, 768), BF16)
    full = jax.ShapeDtypeStruct((256, 768), BF16)
    return pl.pallas_call(
        kernel,
        out_shape=(blk, blk, full, full, full, full),
        in_specs=[vm, vm, vm, hbm, hbm],
        out_specs=(vm,) * 6,
        scratch_shapes=[
            V((3, 32, 8, 768), BF16), V((768, 768), BF16), V((768, 768), BF16),
            V((3, 8, 2, 16, 768), F32), V((3, 8, 2, 16, 768), BF16), V((3, 8, 16, 768), BF16),
            V((3, 8, 16, 768), F32), V((3, 8, 16, 768), BF16), V((3, 8, 16, 768), BF16),
            V((3, 8, 2, 16, 768), BF16),
            V((2, 2, 16, 8, 768), F32), V((2, 2, 16, 8, 768), BF16), V((2, 16, 8, 768), BF16),
            V((2, 4, 4, 8, 768), F32), V((2, 4, 4, 8, 768), BF16), V((2, 3, 4, 8, 768), BF16),
            V((2, 4, 8, 768), F32), V((2, 4, 8, 768), BF16), V((2, 4, 8, 768), BF16),
            D(2), D(2, 9, 4), D(2, 9, 4), D(3, 16), D(3, 16), D(3),
            D(3), D(3), D(3, 8), D(3, 8), D(3, 8), D(3, 8), D(3, 8), D(3, 8),
            D(2), D(2), D(2, 3), D(2, 3), D(2, 4), D(2, 4),
        ],
        compiler_params=pltpu.CompilerParams(
            collective_id=0, has_side_effects=True, vmem_limit_bytes=56 * 1024 * 1024
        ),
        name="ffn",
    )(past, grad, tok, win, wout)


def local(tokens, past_tokens, out_grad, w_in, w_out):
    lay, ing, past_all, grad_all, act_all, hid_all = call(past_tokens, out_grad, tokens, w_in, w_out)
    tn = (((0,), (0,)), ((), ()))
    grad_w_out = lax.dot_general(act_all, grad_all, tn, preferred_element_type=F32).astype(BF16)
    grad_w_in = lax.dot_general(past_all, hid_all, tn, preferred_element_type=F32).astype(BF16)
    return (lay, ing, grad_w_in, grad_w_out)


def solution(mesh):
    return jax.shard_map(
        local,
        mesh=mesh,
        in_specs=(P("row", "col"), P("row", "col"), P("row", "col"), P("col", "row"), P("row", "col")),
        out_specs=(P("row", "col"), P("row", "col"), P("col", "row"), P("row", "col")),
        check_vma=False,
    )
```

time: 315 us -> 98.9 us (0.31)
  the two profiles are of different devices: /device:TPU:1 before, /device:TPU:2 now
where the time goes in v1:
time: 98.9 us; the launch traced here: 98.7 us
  Pallas kernels  92.5 us (94%)
  matrix products  4.25 us (4%)
  local copies, waits for them, and re-layouts  1.22 us (1%)
    pallas_call x1, Pallas kernels, call(): pl.pallas_call(kernel, out_shape=(blk, blk, full, full, full, full), in_s...  92.5 us
    dot_general x1, matrix products, local(): lax.dot_general(past_all, hid_all, tn, preferred_element_type=F32)  2.72 us

profile of v1, /device:TPU:2, one launch (start us, length us, event | category | flops | bytes accessed | tf_op | source)
XLA Modules:
  0.0 98.7 jit_solution(8461756248453175144)
XLA Ops:
  0.6 92.5 %ffn.1 = (bf16[8,768]{1,0:T(8,128)(2,1)}, bf16[8,768]{1,0:T(8,128)(2,1)}, bf16[256,768]{1,0:T(8,128)(2,1)}, bf16[256,768]{1,0:T(8,128)(2,1)}, bf16[256,768]{1,0:T(8,128)(2,1)}, /*index=5*/bf16[256,768]{1,0:T(8,128)(2,1)}) custom-call(bf16[8,768]{1,0:T(8,128)(2,1)} %past_ref.1, bf16[8,768]{1,0:T(8,128)(2,1)} %grad_ref.1, bf16[8,768]{1,0:T(8,128)(2,1)} %tok_ref.1, ...), custom_call_target="tpu_custom_call" | custom-call | tf_op jit(solution)/shard_map/ffn/pallas_call | solution.py:283
  93.2 0.0 copy-start
  93.2 0.0 copy-start.1
  93.2 2.7 %convolution_convert_fusion.1 = bf16[768,768]{1,0:T(8,128)(2,1)} fusion(bf16[256,768]{1,0:T(8,128)(2,1)} %get-tuple-element.12, bf16[256,768]{1,0:T(8,128)(2,1)} %get-tuple-element.13), kind=kOutput, calls=%fused_computation.1 | convolution fusion | flops 302579712 | bytes 1966080 | tf_op jit(solution)/shard_map/dot_general | solution.py:311
  95.9 0.0 copy-done
  95.9 0.0 copy-done.1
  95.9 0.0 copy-start.3
  95.9 0.0 copy-start.2
  95.9 1.5 %convolution_convert_fusion = bf16[768,768]{1,0:T(8,128)(2,1)} fusion(bf16[256,768]{1,0:T(8,128)(2,1)S(1)} %copy-done.1, bf16[256,768]{1,0:T(8,128)(2,1)S(1)} %copy-done), kind=kOutput, calls=%fused_computation | convolution fusion | flops 302579712 | bytes 1966080 | tf_op jit(solution)/shard_map/dot_general | solution.py:310
  97.5 0.0 copy-done.3
  97.5 0.6 copy.11
  98.1 0.0 copy-done.2
  98.1 0.6 copy.12
Async XLA Ops:
  93.2 2.7 %copy-start = (bf16[256,768]{1,0:T(8,128)(2,1)S(1)}, bf16[256,768]{1,0:T(8,128)(2,1)}, u32[]{:S(2)}) copy-start(bf16[256,768]{1,0:T(8,128)(2,1)} %get-tuple-element.15) | copy-start | bytes 1179652
  93.2 2.7 %copy-start.1 = (bf16[256,768]{1,0:T(8,128)(2,1)S(1)}, bf16[256,768]{1,0:T(8,128)(2,1)}, u32[]{:S(2)}) copy-start(bf16[256,768]{1,0:T(8,128)(2,1)} %get-tuple-element.14) | copy-start | bytes 1179652
  95.9 1.5 %copy-start.3 = (bf16[8,768]{1,0:T(8,128)(2,1)S(1)}, bf16[8,768]{1,0:T(8,128)(2,1)}, u32[]{:S(2)}) copy-start(bf16[8,768]{1,0:T(8,128)(2,1)} %get-tuple-element.20) | copy-start | bytes 36868
  95.9 2.1 %copy-start.2 = (bf16[8,768]{1,0:T(8,128)(2,1)S(1)}, bf16[8,768]{1,0:T(8,128)(2,1)}, u32[]{:S(2)}) copy-start(bf16[8,768]{1,0:T(8,128)(2,1)} %get-tuple-element.21) | copy-start | bytes 36868

commit v2 on v1

v2 whole, which is shorter than its diff:
```python
import functools

import jax
import jax.numpy as jnp
from jax import lax
from jax.experimental import pallas as pl
from jax.experimental.pallas import tpu as pltpu
from jax.sharding import PartitionSpec as P

MESH = pl.DeviceIdType.MESH
F32, BF16 = jnp.float32, jnp.bfloat16
NZ = 16


def gelu_parts(pre):
    cdf = 0.5 * (1.0 + lax.erf(pre * 0.7071067811865476))
    slope = cdf + pre * jnp.exp(-0.5 * pre * pre) * 0.3989422804014327
    return (pre * cdf, slope)


SEED = (0, 4, -4, 8)
SPREAD = ((1, 0), (-1, 0), (2, 0), (-2, 0), (1, 1), (-1, 1), (2, 1), (1, 2), (-1, 2), (-2, 2), (1, 3), (-1, 3))


def kernel(
    past_hbm, grad_hbm, tok_hbm, win_hbm, wout_hbm,
    lay_ref, ing_ref, gwi, gwo,
    T, win, wout, Pf, Dr, S8, Cs, Cr, H,
    Rf, Xb, Xr, Sf, Sb, R1, Uf, Ub, R2,
    wsem, ass, asr, bss, bsr, axs, axr, lsem,
    dss, drs, css, crs, hss, hrs, hds, hdr,
    xss, xrs, s1s, s1r, s2s, s2r,
):
    r, q = lax.axis_index("row"), lax.axis_index("col")
    xl, z = r // NZ, r % NZ
    ch, c = q // 2, q % 2
    xh, y = ch // 4, ch % 4
    xp = (1 - xl) * NZ + z
    qp = ch * 2 + (1 - c)
    last = []

    def zrow(d, x=xl):
        return x * NZ + (z + d + 2 * NZ) % NZ

    def chip(k, sign=1):
        return ((xh + sign * (k // 4) + 2) % 2) * 4 + (y + sign * (k % 4) + 4) % 4

    def rcopy(src, dst, ss, rs, rr, qq):
        return pltpu.make_async_remote_copy(
            src_ref=src, dst_ref=dst, send_sem=ss, recv_sem=rs, device_id=(rr, qq), device_id_type=MESH
        )

    def go(cp):
        cp.start()
        last.append(cp.wait_send)

    own = (past_hbm, grad_hbm, tok_hbm)
    locs = [pltpu.make_async_copy(own[a], T.at[a, r], lsem.at[a]) for a in range(3)]
    for cp in locs:
        cp.start()
    cw1 = pltpu.make_async_copy(win_hbm, win, wsem.at[0])
    cw2 = pltpu.make_async_copy(wout_hbm, wout, wsem.at[1])
    cw1.start()
    cw2.start()

    barrier = pltpu.get_barrier_semaphore()
    rows = [zrow(d) for d in (1, -1, 2, -2, 4, -4)] + [xp]
    for rr in rows:
        pl.semaphore_signal(barrier, inc=1, device_id=(rr, q), device_id_type=MESH)
    for qq in [chip(k) * 2 + c for k in range(1, 8)] + [qp]:
        pl.semaphore_signal(barrier, inc=1, device_id=(r, qq), device_id_type=MESH)
    pl.semaphore_wait(barrier, 15)

    def xcopy(src, a, d):
        zz = (z + d + 2 * NZ) % NZ
        slot = xl * NZ + zz
        return rcopy(src, T.at[a, slot], axs.at[a, zz], axr.at[a, zz], xp, q)

    def acopy(src, a, e, e2, d):
        slot = zrow(SEED[e])
        return rcopy(src, T.at[a, slot], ass.at[a, e2], asr.at[a, e2], zrow(d), q)

    def arecv(a, e2):
        slot = zrow(SEED[e2])
        acopy(T.at[a, slot], a, e2, e2, 4).wait_recv()

    def bcopy(src, a, i):
        d, e = SPREAD[i]
        slot = zrow(SEED[e])
        return rcopy(src, T.at[a, slot], bss.at[a, i], bsr.at[a, i], zrow(-d), q)

    def brecv(a, i):
        d, e = SPREAD[i]
        slot = zrow(d + SEED[e])
        rcopy(T.at[a, slot], T.at[a, slot], bss.at[a, i], bsr.at[a, i], zrow(-d), q).wait_recv()
        go(xcopy(T.at[a, slot], a, d + SEED[e]))

    def seeded(a, e):
        src = T.at[a, zrow(SEED[e])]
        if e == 0:
            go(acopy(src, a, 0, 1, -4))
            go(acopy(src, a, 0, 2, 4))
        far = 1 + a % 2
        if e == far:
            go(acopy(src, a, e, 3, -SEED[e]))
        for i, (d, e2) in enumerate(SPREAD):
            if e2 == e:
                go(bcopy(src, a, i))
        go(xcopy(src, a, SEED[e]))

    def spread_of(a, es):
        for i, (d, e) in enumerate(SPREAD):
            if e in es:
                brecv(a, i)

    for a in range(3):
        locs[a].wait()
        seeded(a, 0)
    for a in range(3):
        spread_of(a, (0,))
    for a in range(3):
        for e in (1, 2):
            arecv(a, e)
            seeded(a, e)
    for a in range(3):
        arecv(a, 3)
        seeded(a, 3)
    for a in range(2):
        spread_of(a, (1, 2))
    for a in range(2):
        spread_of(a, (3,))

    cw1.wait()
    cw2.wait()

    def gathered(a):
        @pl.loop(0, NZ)
        def _(zz):
            slot = (1 - xl) * NZ + zz
            rcopy(T.at[a, slot], T.at[a, slot], axs.at[a, zz], axr.at[a, zz], xp, q).wait_recv()

        return T[a].astype(F32).reshape(256, 768).astype(BF16)

    def d2d(k):
        return rcopy(Pf.at[k, :, 1 - c], Dr.at[k], dss.at[k], drs.at[k], r, qp)

    def partial(k, part):
        Pf[k] = part.reshape(8, 2, 16, 768)
        go(d2d(k))

    def csend(k, j):
        return rcopy(Cs.at[k, chip(j)], Cr.at[k, j], css.at[k, j], crs.at[k, j], r, chip(j) * 2 + c)

    def scatter(k):
        d2d(k).wait_recv()
        sums = Pf[k, :, c] + Dr[k]
        S8[k] = sums
        Cs[k] = sums.astype(BF16)
        for j in (6, 2, 4, 5, 7, 1, 3):
            go(csend(k, j))

    def summed(k):
        total = S8[k, ch]
        for j in range(1, 8):
            csend(k, j).wait_recv()
        for j in range(1, 8):
            total = total + Cr[k, j].astype(F32)
        return total

    def hcopy(k, owner, j, ss, rs, core, qq):
        ref = H.at[k, owner, core]
        return rcopy(ref, ref, ss.at[k, j], rs.at[k, j], r, qq)

    def spread(k, value):
        H[k, ch, c] = value
        for j in (6, 2, 4, 5, 7, 1, 3):
            go(hcopy(k, ch, j, hss, hrs, c, chip(j) * 2 + c))
        go(hcopy(k, ch, 0, hds, hdr, c, qp))

    def pass_on(k):
        for j in (1, 3, 4, 2, 5, 7, 6):
            hcopy(k, chip(j, -1), j, hss, hrs, c, qp).wait_recv()
            go(hcopy(k, chip(j, -1), j, hds, hdr, c, qp))

    def whole(k):
        for j in range(8):
            hcopy(k, chip(j, -1), j, hds, hdr, 1 - c, qp).wait_recv()
        return H[k].reshape(256, 768)

    def xsend(k):
        return rcopy(Xb.at[k, 1 - xl], Xr.at[k], xss.at[k], xrs.at[k], xp, q)

    def rpartial(k, part):
        part = part.reshape(2, NZ, 8, 768)
        Rf[k] = part
        Xb[k] = part.astype(BF16)
        go(xsend(k))

    STEP1 = ((2, 1, -1), (-2, 1, -1))

    def send1(k, i):
        d = STEP1[k][i]
        return rcopy(Sb.at[k, :, (z + d + NZ) % 4], R1.at[k, i], s1s.at[k, i], s1r.at[k, i], zrow(d), q)

    def row1(k):
        xsend(k).wait_recv()
        s = Rf[k, xl] + Xr[k].astype(F32)
        s = s.reshape(4, 4, 8, 768)
        Sf[k] = s
        Sb[k] = s.astype(BF16)
        for i in range(3):
            go(send1(k, i))

    def send2(k, i):
        d = 4 * i
        return rcopy(Ub.at[k, ((z + d) % NZ) // 4], R2.at[k, i], s2s.at[k, i], s2r.at[k, i], zrow(d), q)

    def row2(k):
        u = Sf[k, :, z % 4]
        for i in range(3):
            send1(k, i).wait_recv()
        for i in range(3):
            u = u + R1[k, i].astype(F32)
        Uf[k] = u
        Ub[k] = u.astype(BF16)
        for i in (2, 1, 3):
            go(send2(k, i))

    def row3(k, out_ref):
        v = Uf[k, z // 4]
        for i in range(1, 4):
            send2(k, i).wait_recv()
        for i in range(1, 4):
            v = v + R2[k, i].astype(F32)
        out_ref[...] = v.astype(BF16)

    tn = (((0,), (0,)), ((), ()))
    nt = (((1,), (1,)), ((), ()))
    x = gathered(0)
    partial(0, jnp.dot(x, win[...], preferred_element_type=F32))
    g = gathered(1)
    partial(1, lax.dot_general(g, wout[...], nt, preferred_element_type=F32))
    spread_of(2, (1, 2))
    scatter(0)
    scatter(1)
    spread_of(2, (3,))
    partial(2, jnp.dot(gathered(2), win[...], preferred_element_type=F32))
    act, slope = gelu_parts(summed(0))
    spread(0, act.astype(BF16))
    spread(1, (summed(1) * slope).astype(BF16))
    scatter(2)
    pass_on(0)
    pass_on(1)
    spread(2, gelu_parts(summed(2))[0].astype(BF16))
    h = whole(1)
    rpartial(0, lax.dot_general(h, win[...], nt, preferred_element_type=F32))
    pass_on(2)
    rpartial(1, jnp.dot(whole(2), wout[...], preferred_element_type=F32))
    gwi[...] = lax.dot_general(
        T[0].astype(F32).reshape(256, 768).astype(BF16), h, tn, preferred_element_type=F32
    ).astype(BF16)
    row1(0)
    gwo[...] = lax.dot_general(
        whole(0), T[1].astype(F32).reshape(256, 768).astype(BF16), tn, preferred_element_type=F32
    ).astype(BF16)
    row1(1)
    row2(0)
    row2(1)
    row3(0, ing_ref)
    row3(1, lay_ref)

    for wait in last:
        wait()


def call(past, grad, tok, win, wout):
    vm = pl.BlockSpec(memory_space=pltpu.VMEM)
    hbm = pl.BlockSpec(memory_space=pltpu.HBM)
    V = pltpu.VMEM
    D = lambda *s: pltpu.SemaphoreType.DMA(s)
    blk = jax.ShapeDtypeStruct((8, 768), BF16)
    wt = jax.ShapeDtypeStruct((768, 768), BF16)
    return pl.pallas_call(
        kernel,
        out_shape=(blk, blk, wt, wt),
        in_specs=[hbm] * 5,
        out_specs=(vm,) * 4,
        scratch_shapes=[
            V((3, 32, 8, 768), BF16), V((768, 768), BF16), V((768, 768), BF16),
            V((3, 8, 2, 16, 768), F32), V((3, 8, 16, 768), F32),
            V((3, 8, 16, 768), F32), V((3, 8, 16, 768), BF16), V((3, 8, 16, 768), BF16),
            V((3, 8, 2, 16, 768), BF16),
            V((2, 2, 16, 8, 768), F32), V((2, 2, 16, 8, 768), BF16), V((2, 16, 8, 768), BF16),
            V((2, 4, 4, 8, 768), F32), V((2, 4, 4, 8, 768), BF16), V((2, 3, 4, 8, 768), BF16),
            V((2, 4, 8, 768), F32), V((2, 4, 8, 768), BF16), V((2, 4, 8, 768), BF16),
            D(2), D(3, 4), D(3, 4), D(3, 12), D(3, 12), D(3, 16), D(3, 16), D(3),
            D(3), D(3), D(3, 8), D(3, 8), D(3, 8), D(3, 8), D(3, 8), D(3, 8),
            D(2), D(2), D(2, 3), D(2, 3), D(2, 4), D(2, 4),
        ],
        compiler_params=pltpu.CompilerParams(
            collective_id=0, has_side_effects=True, vmem_limit_bytes=36 * 1024 * 1024
        ),
        name="ffn",
    )(past, grad, tok, win, wout)


def local(tokens, past_tokens, out_grad, w_in, w_out):
    return call(past_tokens, out_grad, tokens, w_in, w_out)


def solution(mesh):
    return jax.shard_map(
        local,
        mesh=mesh,
        in_specs=(P("row", "col"), P("row", "col"), P("row", "col"), P("col", "row"), P("row", "col")),
        out_specs=(P("row", "col"), P("row", "col"), P("col", "row"), P("row", "col")),
        check_vma=False,
    )
```

time: 98.9 us -> 92.5 us (0.935)
  the two profiles are of different devices: /device:TPU:2 before, /device:TPU:1 now
where the time goes in v2:
time: 92.5 us; the launch traced here: 92.1 us
  Pallas kernels  83.6 us (90%)
  local copies, waits for them, and re-layouts  7.88 us (9%)
    pallas_call x1, Pallas kernels, call(): pl.pallas_call(kernel, out_shape=(blk, blk, wt, wt), in_specs=[hbm] * 5,...  83.6 us
    unnamed x14, local copies, waits for them, and re-layouts  7.88 us

profile of v2, /device:TPU:1, one launch (start us, length us, event | category | flops | bytes accessed | tf_op | source)
XLA Modules:
  0.0 92.1 jit_solution(4032523546042564631)
XLA Ops:
  0.6 0.0 copy-start
  0.6 1.3 %copy-done = bf16[768,768]{1,0:T(8,128)(2,1)S(1)} copy-done((bf16[768,768]{1,0:T(8,128)(2,1)S(1)}, bf16[768,768]{1,0:T(8,128)(2,1)}, u32[]{:S(2)}) %copy-start) | copy-done | bytes 1179672
  1.9 0.0 copy-start.1
  1.9 1.3 %copy-done.1 = bf16[768,768]{1,0:T(8,128)(2,1)S(1)} copy-done((bf16[768,768]{1,0:T(8,128)(2,1)S(1)}, bf16[768,768]{1,0:T(8,128)(2,1)}, u32[]{:S(2)}) %copy-start.1) | copy-done | bytes 1179672
  3.2 0.0 copy-start.2
  3.2 0.7 copy-done.2
  3.9 0.0 copy-start.3
  3.9 0.7 copy-done.3
  4.6 0.0 copy-start.4
  4.6 0.7 copy-done.4
  5.3 83.6 %ffn.1 = (bf16[8,768]{1,0:T(8,128)(2,1)S(1)}, bf16[8,768]{1,0:T(8,128)(2,1)S(1)}, bf16[768,768]{1,0:T(8,128)(2,1)S(1)}, bf16[768,768]{1,0:T(8,128)(2,1)S(1)}) custom-call(bf16[8,768]{1,0:T(8,128)(2,1)S(1)} %copy-done.2, bf16[8,768]{1,0:T(8,128)(2,1)S(1)} %copy-done.3, bf16[8,768]{1,0:T(8,128)(2,1)S(1)} %copy-done.4, bf16[768,768]{1,0:T(8,128)(2,1)S(1)} %copy-done, ...), custom_call_target="tpu_custom_call" | custom-call | tf_op jit(solution)/shard_map/ffn/pallas_call | solution.py:283
  88.9 0.6 copy.13
  89.5 0.6 copy.14
  90.1 1.0 %copy.15 = bf16[768,768]{1,0:T(8,128)(2,1)} copy(bf16[768,768]{1,0:T(8,128)(2,1)S(1)} %get-tuple-element.10) | data formatting | bytes 2359296
  91.1 1.0 %copy.16 = bf16[768,768]{1,0:T(8,128)(2,1)} copy(bf16[768,768]{1,0:T(8,128)(2,1)S(1)} %get-tuple-element.11) | data formatting | bytes 2359296
Async XLA Ops:
  0.6 1.3 %copy-start = (bf16[768,768]{1,0:T(8,128)(2,1)S(1)}, bf16[768,768]{1,0:T(8,128)(2,1)}, u32[]{:S(2)}) copy-start(bf16[768,768]{1,0:T(8,128)(2,1)} %win_hbm.1) | copy-start | bytes 3538948
  1.9 1.3 %copy-start.1 = (bf16[768,768]{1,0:T(8,128)(2,1)S(1)}, bf16[768,768]{1,0:T(8,128)(2,1)}, u32[]{:S(2)}) copy-start(bf16[768,768]{1,0:T(8,128)(2,1)} %wout_hbm.1) | copy-start | bytes 3538948
  3.2 0.7 copy-start.2
  3.9 0.7 copy-start.3
  4.6 0.7 copy-start.4

commit v3 on v2

--- a/solution.py
+++ b/solution.py
@@ -18,16 +18,20 @@
     return (pre * cdf, slope)
 
 
-SEED = (0, 4, -4, 8)
-SPREAD = ((1, 0), (-1, 0), (2, 0), (-2, 0), (1, 1), (-1, 1), (2, 1), (1, 2), (-1, 2), (-2, 2), (1, 3), (-1, 3))
+SEED = (0, 5, -5)
+NEAR = tuple((d, e) for e in range(3) for d in (2, -2, 1, -1))
+SPREAD = (NEAR + ((3, 1),), NEAR + ((-3, 2),), NEAR + ((3, 1),))
+BOTH = (12,)
+FOLD = tuple((d, m) for m in (5, -5, 0) for d in (2, -2, 1, -1))
+FOLDS = (((-3, -5),) + FOLD, ((3, 5),) + FOLD)
 
 
 def kernel(
-    past_hbm, grad_hbm, tok_hbm, win_hbm, wout_hbm,
+    acts_ref, win_hbm, wout_hbm,
     lay_ref, ing_ref, gwi, gwo,
     T, win, wout, Pf, Dr, S8, Cs, Cr, H,
-    Rf, Xb, Xr, Sf, Sb, R1, Uf, Ub, R2,
-    wsem, ass, asr, bss, bsr, axs, axr, lsem,
+    Rf, Xb, Xr, Sf, Sb, R1, Ub, R2,
+    wsem, ass, asr, bss, bsr, bds, axs, axr, lsem,
     dss, drs, css, crs, hss, hrs, hds, hdr,
     xss, xrs, s1s, s1r, s2s, s2r,
 ):
@@ -54,22 +58,20 @@
         cp.start()
         last.append(cp.wait_send)
 
-    own = (past_hbm, grad_hbm, tok_hbm)
-    locs = [pltpu.make_async_copy(own[a], T.at[a, r], lsem.at[a]) for a in range(3)]
-    for cp in locs:
-        cp.start()
+    loc = pltpu.make_async_copy(acts_ref, T.at[:, r], lsem.at[0])
+    loc.start()
     cw1 = pltpu.make_async_copy(win_hbm, win, wsem.at[0])
     cw2 = pltpu.make_async_copy(wout_hbm, wout, wsem.at[1])
     cw1.start()
     cw2.start()
 
     barrier = pltpu.get_barrier_semaphore()
-    rows = [zrow(d) for d in (1, -1, 2, -2, 4, -4)] + [xp]
+    rows = [zrow(d) for d in (1, -1, 2, -2, 3, -3, 5, -5)] + [zrow(d, 1 - xl) for d in (0, 2, -2, 3, -3)]
     for rr in rows:
         pl.semaphore_signal(barrier, inc=1, device_id=(rr, q), device_id_type=MESH)
     for qq in [chip(k) * 2 + c for k in range(1, 8)] + [qp]:
         pl.semaphore_signal(barrier, inc=1, device_id=(r, qq), device_id_type=MESH)
-    pl.semaphore_wait(barrier, 15)
+    pl.semaphore_wait(barrier, 21)
 
     def xcopy(src, a, d):
         zz = (z + d + 2 * NZ) % NZ
@@ -82,56 +84,62 @@
 
     def arecv(a, e2):
         slot = zrow(SEED[e2])
-        acopy(T.at[a, slot], a, e2, e2, 4).wait_recv()
+        acopy(T.at[a, slot], a, e2, e2, 5).wait_recv()
 
     def bcopy(src, a, i):
-        d, e = SPREAD[i]
+        d, e = SPREAD[a][i]
         slot = zrow(SEED[e])
         return rcopy(src, T.at[a, slot], bss.at[a, i], bsr.at[a, i], zrow(-d), q)
 
+    def bcross(src, a, i):
+        d, e = SPREAD[a][i]
+        zz = (z + SEED[e] + 2 * NZ) % NZ
+        slot = zrow(SEED[e])
+        return rcopy(src, T.at[a, slot], bds.at[a, i], axr.at[a, zz], zrow(-d, 1 - xl), q)
+
     def brecv(a, i):
-        d, e = SPREAD[i]
+        d, e = SPREAD[a][i]
         slot = zrow(d + SEED[e])
         rcopy(T.at[a, slot], T.at[a, slot], bss.at[a, i], bsr.at[a, i], zrow(-d), q).wait_recv()
-        go(xcopy(T.at[a, slot], a, d + SEED[e]))
+        if i not in BOTH:
+            go(xcopy(T.at[a, slot], a, d + SEED[e]))
 
     def seeded(a, e):
-        src = T.at[a, zrow(SEED[e])]
+        src = acts_ref.at[a] if e == 0 else T.at[a, zrow(SEED[e])]
         if e == 0:
-            go(acopy(src, a, 0, 1, -4))
-            go(acopy(src, a, 0, 2, 4))
-        far = 1 + a % 2
-        if e == far:
-            go(acopy(src, a, e, 3, -SEED[e]))
-        for i, (d, e2) in enumerate(SPREAD):
-            if e2 == e:
+            go(acopy(src, a, 0, 1, -5))
+            go(acopy(src, a, 0, 2, 5))
+        for i in sorted(range(13), key=lambda i: -abs(SPREAD[a][i][0])):
+            if SPREAD[a][i][1] == e:
                 go(bcopy(src, a, i))
+                if i in BOTH:
+                    go(bcross(src, a, i))
         go(xcopy(src, a, SEED[e]))
 
     def spread_of(a, es):
-        for i, (d, e) in enumerate(SPREAD):
+        for i, (d, e) in enumerate(SPREAD[a]):
             if e in es:
                 brecv(a, i)
 
-    for a in range(3):
-        locs[a].wait()
+    for a in range(2):
         seeded(a, 0)
-    for a in range(3):
+    for a in range(2):
         spread_of(a, (0,))
-    for a in range(3):
+    for a in range(2):
         for e in (1, 2):
             arecv(a, e)
             seeded(a, e)
-    for a in range(3):
-        arecv(a, 3)
-        seeded(a, 3)
+    seeded(2, 0)
     for a in range(2):
         spread_of(a, (1, 2))
-    for a in range(2):
-        spread_of(a, (3,))
+    spread_of(2, (0,))
+    for e in (1, 2):
+        arecv(2, e)
+        seeded(2, e)
 
     cw1.wait()
     cw2.wait()
+    loc.wait()
 
     def gathered(a):
         @pl.loop(0, NZ)
@@ -196,41 +204,40 @@
         Xb[k] = part.astype(BF16)
         go(xsend(k))
 
-    STEP1 = ((2, 1, -1), (-2, 1, -1))
-
     def send1(k, i):
-        d = STEP1[k][i]
-        return rcopy(Sb.at[k, :, (z + d + NZ) % 4], R1.at[k, i], s1s.at[k, i], s1r.at[k, i], zrow(d), q)
+        d, m = FOLDS[k][i]
+        return rcopy(Sb.at[k, (z + d + m + NZ) % NZ], R1.at[k, i], s1s.at[k, i], s1r.at[k, i], zrow(d), q)
 
     def row1(k):
         xsend(k).wait_recv()
         s = Rf[k, xl] + Xr[k].astype(F32)
-        s = s.reshape(4, 4, 8, 768)
         Sf[k] = s
         Sb[k] = s.astype(BF16)
-        for i in range(3):
+        for i in range(13):
             go(send1(k, i))
 
+    def folded(k, m):
+        u = Sf[k, (z + m + NZ) % NZ]
+        mine = [i for i in range(13) if FOLDS[k][i][1] == m]
+        for i in mine:
+            send1(k, i).wait_recv()
+        for i in mine:
+            u = u + R1[k, i].astype(F32)
+        return u
+
     def send2(k, i):
-        d = 4 * i
-        return rcopy(Ub.at[k, ((z + d) % NZ) // 4], R2.at[k, i], s2s.at[k, i], s2r.at[k, i], zrow(d), q)
+        return rcopy(Ub.at[k, i], R2.at[k, i], s2s.at[k, i], s2r.at[k, i], zrow(5 - 10 * i), q)
 
     def row2(k):
-        u = Sf[k, :, z % 4]
-        for i in range(3):
-            send1(k, i).wait_recv()
-        for i in range(3):
-            u = u + R1[k, i].astype(F32)
-        Uf[k] = u
-        Ub[k] = u.astype(BF16)
-        for i in (2, 1, 3):
+        for i in range(2):
+            Ub[k, i] = folded(k, 5 - 10 * i).astype(BF16)
             go(send2(k, i))
 
     def row3(k, out_ref):
-        v = Uf[k, z // 4]
-        for i in range(1, 4):
+        v = folded(k, 0)
+        for i in range(2):
             send2(k, i).wait_recv()
-        for i in range(1, 4):
+        for i in range(2):
             v = v + R2[k, i].astype(F32)
         out_ref[...] = v.astype(BF16)
 
@@ -240,10 +247,9 @@
     partial(0, jnp.dot(x, win[...], preferred_element_type=F32))
     g = gathered(1)
     partial(1, lax.dot_general(g, wout[...], nt, preferred_element_type=F32))
-    spread_of(2, (1, 2))
     scatter(0)
     scatter(1)
-    spread_of(2, (3,))
+    spread_of(2, (1, 2))
     partial(2, jnp.dot(gathered(2), win[...], preferred_element_type=F32))
     act, slope = gelu_parts(summed(0))
     spread(0, act.astype(BF16))
@@ -273,7 +279,7 @@
         wait()
 
 
-def call(past, grad, tok, win, wout):
+def call(acts, win, wout):
     vm = pl.BlockSpec(memory_space=pltpu.VMEM)
     hbm = pl.BlockSpec(memory_space=pltpu.HBM)
     V = pltpu.VMEM
@@ -283,7 +289,7 @@
     return pl.pallas_call(
         kernel,
         out_shape=(blk, blk, wt, wt),
-        in_specs=[hbm] * 5,
+        in_specs=[vm, hbm, hbm],
         out_specs=(vm,) * 4,
         scratch_shapes=[
             V((3, 32, 8, 768), BF16), V((768, 768), BF16), V((768, 768), BF16),
@@ -291,21 +297,21 @@
             V((3, 8, 16, 768), F32), V((3, 8, 16, 768), BF16), V((3, 8, 16, 768), BF16),
             V((3, 8, 2, 16, 768), BF16),
             V((2, 2, 16, 8, 768), F32), V((2, 2, 16, 8, 768), BF16), V((2, 16, 8, 768), BF16),
-            V((2, 4, 4, 8, 768), F32), V((2, 4, 4, 8, 768), BF16), V((2, 3, 4, 8, 768), BF16),
-            V((2, 4, 8, 768), F32), V((2, 4, 8, 768), BF16), V((2, 4, 8, 768), BF16),
-            D(2), D(3, 4), D(3, 4), D(3, 12), D(3, 12), D(3, 16), D(3, 16), D(3),
+            V((2, 16, 8, 768), F32), V((2, 16, 8, 768), BF16), V((2, 13, 8, 768), BF16),
+            V((2, 2, 8, 768), BF16), V((2, 2, 8, 768), BF16),
+            D(2), D(3, 3), D(3, 3), D(3, 13), D(3, 13), D(3, 13), D(3, 16), D(3, 16), D(1),
             D(3), D(3), D(3, 8), D(3, 8), D(3, 8), D(3, 8), D(3, 8), D(3, 8),
-            D(2), D(2), D(2, 3), D(2, 3), D(2, 4), D(2, 4),
+            D(2), D(2), D(2, 13), D(2, 13), D(2, 2), D(2, 2),
         ],
         compiler_params=pltpu.CompilerParams(
-            collective_id=0, has_side_effects=True, vmem_limit_bytes=36 * 1024 * 1024
+            collective_id=0, has_side_effects=True, vmem_limit_bytes=51 * 1024 * 1024
         ),
         name="ffn",
-    )(past, grad, tok, win, wout)
+    )(acts, win, wout)
 
 
 def local(tokens, past_tokens, out_grad, w_in, w_out):
-    return call(past_tokens, out_grad, tokens, w_in, w_out)
+    return call(jnp.stack((past_tokens, out_grad, tokens)), w_in, w_out)
 
 
 def solution(mesh):

time: 92.5 us -> 83.7 us (0.905)
  Pallas kernels: 83.6 us -> 78.8 us
  local copies, waits for them, and re-layouts: 7.88 us -> 3.23 us
    pallas_call x1, Pallas kernels: 83.6 us -> 78.8 us  [call(): pl.pallas_call(kernel, out_shape=(blk, blk, wt, wt), in_specs=[vm, hbm, h...]
    unnamed x14 -> x4, local copies, waits for them, and re-layouts: 7.88 us -> 3.23 us
where the time goes in v3:
time: 83.7 us; the launch traced here: 83.4 us
  Pallas kernels  78.8 us (94%)
  local copies, waits for them, and re-layouts  3.23 us (4%)
    pallas_call x1, Pallas kernels, call(): pl.pallas_call(kernel, out_shape=(blk, blk, wt, wt), in_specs=[vm, hbm, h...  78.8 us
    unnamed x4, local copies, waits for them, and re-layouts  3.23 us

profile of v3, /device:TPU:1, one launch (start us, length us, event | category | flops | bytes accessed | tf_op | source)
XLA Modules:
  0.0 83.4 jit_solution(9580924025055869517)
XLA Ops:
  0.6 0.7 pad_maximum_fusion.acts_ref
  1.4 78.8 %ffn.1 = (bf16[8,768]{1,0:T(8,128)(2,1)S(1)}, bf16[8,768]{1,0:T(8,128)(2,1)S(1)}, bf16[768,768]{1,0:T(8,128)(2,1)S(1)}, bf16[768,768]{1,0:T(8,128)(2,1)S(1)}) custom-call(bf16[3,8,768]{2,1,0:T(8,128)(2,1)S(1)} %pad_maximum_fusion.acts_ref, bf16[768,768]{1,0:T(8,128)(2,1)} %win_hbm.1, bf16[768,768]{1,0:T(8,128)(2,1)} %wout_hbm.1), custom_call_target="tpu_custom_call" | custom-call | tf_op jit(solution)/shard_map/ffn/pallas_call | solution.py:289
  80.2 0.6 copy.13
  80.8 0.6 copy.14
  81.4 1.0 %copy.15 = bf16[768,768]{1,0:T(8,128)(2,1)} copy(bf16[768,768]{1,0:T(8,128)(2,1)S(1)} %get-tuple-element.10) | data formatting | bytes 2359296
  82.4 1.0 %copy.16 = bf16[768,768]{1,0:T(8,128)(2,1)} copy(bf16[768,768]{1,0:T(8,128)(2,1)S(1)} %get-tuple-element.11) | data formatting | bytes 2359296

commit v4 on v3

--- a/solution.py
+++ b/solution.py
@@ -21,7 +21,7 @@
 SEED = (0, 5, -5)
 NEAR = tuple((d, e) for e in range(3) for d in (2, -2, 1, -1))
 SPREAD = (NEAR + ((3, 1),), NEAR + ((-3, 2),), NEAR + ((3, 1),))
-BOTH = (12,)
+BOTH = ()
 FOLD = tuple((d, m) for m in (5, -5, 0) for d in (2, -2, 1, -1))
 FOLDS = (((-3, -5),) + FOLD, ((3, 5),) + FOLD)
 
@@ -199,13 +199,14 @@
         return rcopy(Xb.at[k, 1 - xl], Xr.at[k], xss.at[k], xrs.at[k], xp, q)
 
     def rpartial(k, part):
-        part = part.reshape(2, NZ, 8, 768)
-        Rf[k] = part
-        Xb[k] = part.astype(BF16)
-        go(xsend(k))
+        for f in range(2):
+            half = part[:, 384 * f : 384 * f + 384].reshape(2, NZ, 8, 384)
+            Rf[2 * k + f] = half
+            Xb[2 * k + f] = half.astype(BF16)
+            go(xsend(2 * k + f))
 
     def send1(k, i):
-        d, m = FOLDS[k][i]
+        d, m = FOLDS[k % 2][i]
         return rcopy(Sb.at[k, (z + d + m + NZ) % NZ], R1.at[k, i], s1s.at[k, i], s1r.at[k, i], zrow(d), q)
 
     def row1(k):
@@ -218,7 +219,7 @@
 
     def folded(k, m):
         u = Sf[k, (z + m + NZ) % NZ]
-        mine = [i for i in range(13) if FOLDS[k][i][1] == m]
+        mine = [i for i in range(13) if FOLDS[k % 2][i][1] == m]
         for i in mine:
             send1(k, i).wait_recv()
         for i in mine:
@@ -239,7 +240,7 @@
             send2(k, i).wait_recv()
         for i in range(2):
             v = v + R2[k, i].astype(F32)
-        out_ref[...] = v.astype(BF16)
+        out_ref[:, 384 * (k % 2) : 384 * (k % 2) + 384] = v.astype(BF16)
 
     tn = (((0,), (0,)), ((), ()))
     nt = (((1,), (1,)), ((), ()))
@@ -252,28 +253,34 @@
     spread_of(2, (1, 2))
     partial(2, jnp.dot(gathered(2), win[...], preferred_element_type=F32))
     act, slope = gelu_parts(summed(0))
-    spread(0, act.astype(BF16))
     spread(1, (summed(1) * slope).astype(BF16))
     scatter(2)
-    pass_on(0)
     pass_on(1)
     spread(2, gelu_parts(summed(2))[0].astype(BF16))
+    spread(0, act.astype(BF16))
     h = whole(1)
     rpartial(0, lax.dot_general(h, win[...], nt, preferred_element_type=F32))
     pass_on(2)
     rpartial(1, jnp.dot(whole(2), wout[...], preferred_element_type=F32))
+    pass_on(0)
+    row1(0)
+    row1(1)
     gwi[...] = lax.dot_general(
         T[0].astype(F32).reshape(256, 768).astype(BF16), h, tn, preferred_element_type=F32
     ).astype(BF16)
-    row1(0)
+    row1(2)
+    row1(3)
+    row2(0)
+    row2(1)
     gwo[...] = lax.dot_general(
         whole(0), T[1].astype(F32).reshape(256, 768).astype(BF16), tn, preferred_element_type=F32
     ).astype(BF16)
-    row1(1)
-    row2(0)
-    row2(1)
+    row2(2)
+    row2(3)
     row3(0, ing_ref)
-    row3(1, lay_ref)
+    row3(1, ing_ref)
+    row3(2, lay_ref)
+    row3(3, lay_ref)
 
     for wait in last:
         wait()
@@ -296,12 +303,12 @@
             V((3, 8, 2, 16, 768), F32), V((3, 8, 16, 768), F32),
             V((3, 8, 16, 768), F32), V((3, 8, 16, 768), BF16), V((3, 8, 16, 768), BF16),
             V((3, 8, 2, 16, 768), BF16),
-            V((2, 2, 16, 8, 768), F32), V((2, 2, 16, 8, 768), BF16), V((2, 16, 8, 768), BF16),
-            V((2, 16, 8, 768), F32), V((2, 16, 8, 768), BF16), V((2, 13, 8, 768), BF16),
-            V((2, 2, 8, 768), BF16), V((2, 2, 8, 768), BF16),
+            V((4, 2, 16, 8, 384), F32), V((4, 2, 16, 8, 384), BF16), V((4, 16, 8, 384), BF16),
+            V((4, 16, 8, 384), F32), V((4, 16, 8, 384), BF16), V((4, 13, 8, 384), BF16),
+            V((4, 2, 8, 384), BF16), V((4, 2, 8, 384), BF16),
             D(2), D(3, 3), D(3, 3), D(3, 13), D(3, 13), D(3, 13), D(3, 16), D(3, 16), D(1),
             D(3), D(3), D(3, 8), D(3, 8), D(3, 8), D(3, 8), D(3, 8), D(3, 8),
-            D(2), D(2), D(2, 13), D(2, 13), D(2, 2), D(2, 2),
+            D(4), D(4), D(4, 13), D(4, 13), D(4, 2), D(4, 2),
         ],
         compiler_params=pltpu.CompilerParams(
             collective_id=0, has_side_effects=True, vmem_limit_bytes=51 * 1024 * 1024

time: 83.7 us -> 82.3 us (0.983); the launches traced: 83.4 us -> 81.1 us
  Pallas kernels: 78.8 us -> 76.4 us
    pallas_call x1, Pallas kernels: 78.8 us -> 76.4 us  [call(): pl.pallas_call(kernel, out_shape=(blk, blk, wt, wt), in_specs=[vm, hbm, h...]
where the time goes in v4:
time: 82.3 us; the launch traced here: 81.1 us
  Pallas kernels  76.4 us (93%)
  local copies, waits for them, and re-layouts  3.23 us (4%)
    pallas_call x1, Pallas kernels, call(): pl.pallas_call(kernel, out_shape=(blk, blk, wt, wt), in_specs=[vm, hbm, h...  76.4 us
    unnamed x4, local copies, waits for them, and re-layouts  3.23 us

profile of v4, /device:TPU:1, one launch (start us, length us, event | category | flops | bytes accessed | tf_op | source)
XLA Modules:
  0.0 81.1 jit_solution(2468938696759845875)
XLA Ops:
  0.6 0.7 pad_maximum_fusion.acts_ref
  1.4 76.4 %ffn.1 = (bf16[8,768]{1,0:T(8,128)(2,1)S(1)}, bf16[8,768]{1,0:T(8,128)(2,1)S(1)}, bf16[768,768]{1,0:T(8,128)(2,1)S(1)}, bf16[768,768]{1,0:T(8,128)(2,1)S(1)}) custom-call(bf16[3,8,768]{2,1,0:T(8,128)(2,1)S(1)} %pad_maximum_fusion.acts_ref, bf16[768,768]{1,0:T(8,128)(2,1)} %win_hbm.1, bf16[768,768]{1,0:T(8,128)(2,1)} %wout_hbm.1), custom_call_target="tpu_custom_call" | custom-call | tf_op jit(solution)/shard_map/ffn/pallas_call | solution.py:296
  77.8 0.6 copy.13
  78.4 0.6 copy.14
  79.0 1.0 %copy.15 = bf16[768,768]{1,0:T(8,128)(2,1)} copy(bf16[768,768]{1,0:T(8,128)(2,1)S(1)} %get-tuple-element.10) | data formatting | bytes 2359296
  80.0 1.0 %copy.16 = bf16[768,768]{1,0:T(8,128)(2,1)} copy(bf16[768,768]{1,0:T(8,128)(2,1)S(1)} %get-tuple-element.11) | data formatting | bytes 2359296
